TPU v7x, 32 devices: a whole 2x2x4 slice. The times are simulated.
32 devices in a mesh: league: 8 (over z, y), rep: 4 (over x, core).
Axes of the slice: x: 2, y: 2, z: 4, core: 2. Of those that a mesh axis runs over, the one named last changes fastest.
Arguments:
- observations: bfloat16 [4096, 2048], P(('league', 'rep')), may hold values from -6 to 6
- weights: bfloat16 [8, 2048, 2048], P('league', None, 'rep'), may hold values from -0.125 to 0.125
- gains: float32 [8, 2048], P('league'), may hold values from 0.5 to 1.5
- heads: bfloat16 [8, 2048], P('league', 'rep'), may hold values from -0.125 to 0.125
- pairing: int32 [4096, 1], P(('league', 'rep')), may hold values from 0 to 7; in each aligned block of 128 rows (0 to 127, 128 to 255, ...) at most 32 rows name the same one
- valid: int32 [4096], P(('league', 'rep')), may hold values 0 or 1
Outputs:
- own_value: float32 [4096], P(('league', 'rep'))
- opponent_value: float32 [4096], P(('league', 'rep'))
Inputs may be any that keep to these rules, and one draw needn't show every extreme that they name: `pairing`: among the rows of one device, at most 32 name one agent; every agent is named by some row of the whole batch.
All inputs are finite; a program needn't handle non-finite values. No bound on the sum of `valid` on one device may be relied on, other than what follows from the above.
Results may differ from a plain program's by a relative error of at most 0.003.
Values may be sent and summed in bfloat16 or wider, within the bound.
A program may use at most 64 MiB of HBM per device.

v0:
```python
import functools

import jax
import jax.numpy as jnp
from jax import lax
from jax.experimental import pallas as pl
from jax.experimental.pallas import tpu as pltpu
from jax.sharding import PartitionSpec as P

MESH = pl.DeviceIdType.MESH
TILE = 512
PARTS = 4


def normed_values(obs_rows, agent_gain, weight_cols, head_cols):
    wide_rows = obs_rows.astype(jnp.float32)
    squares = jnp.mean(wide_rows * wide_rows, axis=1, keepdims=True)
    scaled = (wide_rows * lax.rsqrt(squares + 1e-06) * agent_gain).astype(jnp.bfloat16)
    hidden = jax.nn.silu(jnp.dot(scaled, weight_cols, preferred_element_type=jnp.float32))
    return jnp.sum(hidden * head_cols.astype(jnp.float32), axis=1)


def gathered_plan(observations, weights, gains, heads, pairing, valid):
    rows_dev, feature_width = observations.shape
    n_league = lax.axis_size("league")
    capacity = max(2, 2 * rows_dev // n_league)
    own_gain = gains[0]
    weight_full = lax.all_gather(weights[0], "rep", axis=1, tiled=True)
    head_full = lax.all_gather(heads[0], "rep", axis=0, tiled=True)
    own_value = normed_values(observations, own_gain, weight_full, head_full)
    owner_id = pairing[:, 0]
    is_live = valid == 1
    agent_iota = jnp.arange(n_league, dtype=jnp.int32)
    pick_table = ((owner_id[:, None] == agent_iota[None, :]) & is_live[:, None]).astype(jnp.float32)
    row_iota = jnp.arange(rows_dev, dtype=jnp.int32)
    earlier = (row_iota[:, None] > row_iota[None, :]).astype(jnp.float32)
    before = jnp.dot(earlier, pick_table, precision=lax.Precision.HIGHEST)
    slot_index = jnp.sum(before * pick_table, axis=1).astype(jnp.int32)
    target = jnp.where(is_live, owner_id * capacity + slot_index, n_league * capacity)
    outgoing = (
        jnp.zeros((n_league * capacity + 1, feature_width), jnp.bfloat16)
        .at[target]
        .set(observations)
    )
    outgoing = outgoing[: n_league * capacity].reshape(n_league, capacity, feature_width)
    received = lax.all_to_all(outgoing, "league", split_axis=0, concat_axis=0, tiled=True)
    flat_rows = received.reshape(received.shape[0] * received.shape[1], feature_width)
    answers = normed_values(flat_rows, own_gain, weight_full, head_full).reshape(
        received.shape[0], received.shape[1]
    )
    returned = lax.all_to_all(answers, "league", split_axis=0, concat_axis=0, tiled=True)
    flat_back = jnp.concatenate([returned.reshape(-1), jnp.zeros((1,), jnp.float32)])
    opponent_value = jnp.where(is_live, flat_back[target], 0.0)
    return (own_value, opponent_value)


def kernel(
    n, cap,
    obs_hbm, w_hbm, gain_ref, head_ref, pair_ref, valid_ref,
    out_ref,
    rows, wbuf, hv, code, slots, taken, scaled, res, back, vown,
    lsem, asem, slot_send, slot_recv, far_send, far_recv, back_send, back_recv,
):
    hs = n // 2
    rd, width = rows.shape[1], rows.shape[2]
    hid = wbuf.shape[2]
    lg = lax.axis_index("league")
    rp = lax.axis_index("rep")
    n_rep = lax.axis_size("rep")
    partner = lax.rem(rp + n_rep // 2, n_rep)
    sibling = rp + 1 - 2 * lax.rem(rp, 2)
    half = lg // hs
    pos = lax.rem(lg, hs)
    far_half = 1 - half

    copy_obs = pltpu.make_async_copy(obs_hbm, rows.at[0], lsem.at[0])
    copy_w = pltpu.make_async_copy(w_hbm, wbuf.at[0], lsem.at[1])
    copy_obs.start()
    copy_w.start()

    barrier = pltpu.get_barrier_semaphore()
    pl.semaphore_signal(barrier, inc=1, device_id=(lg, sibling), device_id_type=MESH)
    pl.semaphore_signal(barrier, inc=1, device_id=(lg, partner), device_id_type=MESH)
    for k in range(1, n):
        other = lax.rem(lg + k, n)
        for who in (rp, partner):
            pl.semaphore_signal(barrier, inc=1, device_id=(other, who), device_id_type=MESH)

    lane = lax.broadcasted_iota(jnp.int32, (rd, rd), 1)
    sub = lax.broadcasted_iota(jnp.int32, (rd, rd), 0)
    agent_sub = lax.broadcasted_iota(jnp.int32, (n, rd), 0)

    def placing(agent):
        pick = jnp.where(agent == agent_sub, 1.0, 0.0)
        earlier = jnp.where(sub < lane, 1.0, 0.0).astype(jnp.bfloat16)
        before = jnp.dot(pick.astype(jnp.bfloat16), earlier, preferred_element_type=jnp.float32)
        slot = jnp.sum(before * pick, axis=0, keepdims=True).astype(jnp.int32)
        return pick, slot

    def fill(which, source, agent, slot, side):
        place = agent * cap + slot - side * rd
        chosen = jnp.where(sub == place, 1.0, 0.0).astype(jnp.bfloat16)
        picked = jnp.dot(chosen, rows[source], preferred_element_type=jnp.float32)
        slots[which] = picked.astype(jnp.bfloat16).reshape(hs, cap, width)

    my_code = jnp.where(valid_ref[...] == 1, pair_ref[...], -1)
    code[0] = my_code
    hv[0] = head_ref[...].astype(jnp.float32)
    my_pick, my_slot = placing(my_code)
    none = jnp.zeros((cap, width), jnp.bfloat16)
    taken[0, pos] = none
    taken[2, pos] = none
    back[0, lg] = jnp.zeros((1, rd), jnp.float32)
    back[1, lg] = jnp.zeros((1, rd), jnp.float32)
    copy_obs.wait()
    fill(1, 0, my_code, my_slot, far_half)
    fill(0, 0, my_code, my_slot, half)
    pl.semaphore_wait(barrier, 2 * n)

    def remote(src, dst, send, recv, to):
        return pltpu.make_async_remote_copy(
            src_ref=src, dst_ref=dst, send_sem=send, recv_sem=recv,
            device_id=to, device_id_type=MESH,
        )

    def ahead(k):
        return lax.rem(pos + k, hs)

    send_code = remote(code.at[0], code.at[1], asem.at[0, 0], asem.at[1, 0], (lg, partner))
    send_rows = remote(rows.at[0], rows.at[1], asem.at[0, 1], asem.at[1, 1], (lg, partner))
    send_head = remote(hv.at[0], hv.at[1], asem.at[0, 2], asem.at[1, 2], (lg, sibling))
    send_w = remote(wbuf.at[0], wbuf.at[1], asem.at[0, 3], asem.at[1, 3], (lg, sibling))
    send_code.start()
    send_rows.start()

    def far_target(j):
        return lax.rem(pos // 2 + 1 + j, 2) * 2 + lax.rem(pos + 1 + j // 2, 2)

    def far_source(j):
        return lax.rem(pos // 2 + 1 + j, 2) * 2 + lax.rem(pos + 1 + j // 2, 2)

    def cut(ref, part):
        span = width // PARTS
        return ref.at[:, pl.ds(part * span, span)]

    def far_copy(j, part):
        to = far_target(j)
        return remote(
            cut(slots.at[1, to], part), cut(taken.at[1, pos], part),
            far_send.at[0, to, part], far_recv.at[0, pos, part], (far_half * hs + to, rp),
        )

    def arrival(j, part):
        q = far_source(j)
        return remote(
            cut(slots.at[1, q], part), cut(taken.at[1, q], part),
            far_send.at[0, q, part], far_recv.at[0, q, part], (far_half * hs + q, rp),
        )

    def forward_copy(j, part):
        q = far_source(j)
        return remote(
            cut(taken.at[1, q], part), cut(taken.at[3, q], part),
            far_send.at[1, q, part], far_recv.at[1, q, part], (lg, partner),
        )

    def near_copy(kind, k):
        return remote(
            slots.at[kind, ahead(k)], taken.at[kind, pos],
            slot_send.at[kind // 2, k], slot_recv.at[kind // 2, k], (half * hs + ahead(k), rp),
        )

    near = {(kind, k): near_copy(kind, k) for kind in (0, 2) for k in range(1, hs)}
    far = [far_copy(j, part) for j in range(hs) for part in range(PARTS)]
    onward = [forward_copy(j, part) for j in range(hs) for part in range(PARTS)]
    for move in far:
        move.start()
    for k in range(1, hs):
        near[0, k].start()
    copy_w.wait()
    send_head.start()
    send_w.start()

    def values(block):
        wide = block.astype(jnp.float32)
        squares = jnp.mean(wide * wide, axis=1, keepdims=True)
        scaled[...] = (wide * lax.rsqrt(squares + 1e-06) * gain_ref[...]).astype(jnp.bfloat16)
        per = hid // TILE

        def tile(i, acc):
            j = i // per
            col = pl.multiple_of(lax.rem(i, per) * TILE, TILE)
            v = jnp.dot(scaled[...], wbuf[j, :, pl.ds(col, TILE)], preferred_element_type=jnp.float32)
            part = v / (1.0 + jnp.exp(-v)) * hv[j, :, pl.ds(col, TILE)]
            for c in range(0, TILE, rd):
                acc = acc + part[:, c:c + rd]
            return acc

        acc = lax.fori_loop(0, 2 * per, tile, jnp.zeros((rd, rd), jnp.float32))
        return jnp.sum(acc.T, axis=0, keepdims=True)

    first = {0: 1, 1: 0, 2: 1, 3: 0}
    replies = {}

    def answer(kind):
        res[kind] = values(taken[kind].reshape(rd, width))
        who = rp if kind < 2 else partner
        side = far_half if kind % 2 == 1 else half
        for k in range(first[kind], hs):
            replies[kind, k] = remote(
                res.at[kind], back.at[kind // 2, lg],
                back_send.at[kind, k], back_recv.at[kind, k],
                (side * hs + ahead(k), who),
            )
            replies[kind, k].start()

    send_head.wait_recv()
    send_w.wait_recv()
    mine = values(rows[0])

    send_code.wait_recv()
    send_rows.wait_recv()
    other_code = code[1]
    fill(2, 1, other_code, placing(other_code)[1], half)
    for k in range(1, hs):
        near[2, k].start()

    def forward(j):
        for part in range(PARTS):
            arrival(j, part).wait_recv()
            onward[j * PARTS + part].start()

    forward(0)
    vown[0] = values(rows[1])
    send_own = remote(vown.at[0], vown.at[1], asem.at[0, 4], asem.at[1, 4], (lg, partner))
    send_own.start()
    forward(1)
    for k in range(1, hs):
        near[0, k].wait_recv()
    answer(0)
    forward(2)
    forward(3)
    for k in range(1, hs):
        near[2, k].wait_recv()
    answer(2)
    answer(1)
    for move in onward:
        move.wait_recv()
    answer(3)

    send_own.wait_recv()
    own = mine + vown[1]
    out_ref[0] = own
    for move in replies.values():
        move.wait_recv()
    table = jnp.concatenate([back[0, a] + back[1, a] for a in range(n)], axis=0)
    spot = lax.broadcasted_iota(jnp.int32, (n, rd), 1) - pos * cap
    table = jnp.where((spot >= 0) & (spot < cap), table, 0.0)
    chosen = jnp.where(sub == my_slot + pos * cap, 1.0, 0.0)
    found = jnp.dot(table, chosen, preferred_element_type=jnp.float32, precision=lax.Precision.HIGHEST)
    opp = jnp.sum(jnp.where(my_pick > 0.0, found, 0.0), axis=0, keepdims=True)
    out_ref[1] = jnp.where(my_code == lg, own, opp)
    for move in [send_code, send_rows, send_head, send_w, send_own, *near.values(), *far, *onward, *replies.values()]:
        move.wait_send()


def kernel_plan(observations, weights, gains, heads, pairing, valid):
    rd, width = observations.shape
    hid = weights.shape[2]
    n = lax.axis_size("league")
    cap = 2 * rd // n
    hs = n // 2
    vmem = pl.BlockSpec(memory_space=pltpu.VMEM)
    anywhere = pl.BlockSpec(memory_space=pl.ANY)
    both = pl.pallas_call(
        functools.partial(kernel, n, cap),
        out_shape=jax.ShapeDtypeStruct((2, 1, rd), jnp.float32),
        in_specs=[anywhere, anywhere, vmem, vmem, vmem, vmem],
        out_specs=vmem,
        scratch_shapes=[
            pltpu.VMEM((2, rd, width), jnp.bfloat16),
            pltpu.VMEM((2, width, hid), jnp.bfloat16),
            pltpu.VMEM((2, 1, hid), jnp.float32),
            pltpu.VMEM((2, 1, rd), jnp.int32),
            pltpu.VMEM((3, hs, cap, width), jnp.bfloat16),
            pltpu.VMEM((4, hs, cap, width), jnp.bfloat16),
            pltpu.VMEM((rd, width), jnp.bfloat16),
            pltpu.VMEM((4, 1, rd), jnp.float32),
            pltpu.VMEM((2, n, 1, rd), jnp.float32),
            pltpu.VMEM((2, 1, rd), jnp.float32),
            pltpu.SemaphoreType.DMA((2,)),
            pltpu.SemaphoreType.DMA((2, 5)),
            pltpu.SemaphoreType.DMA((2, hs)),
            pltpu.SemaphoreType.DMA((2, hs)),
            pltpu.SemaphoreType.DMA((2, hs, PARTS)),
            pltpu.SemaphoreType.DMA((2, hs, PARTS)),
            pltpu.SemaphoreType.DMA((4, hs)),
            pltpu.SemaphoreType.DMA((4, hs)),
        ],
        compiler_params=pltpu.CompilerParams(collective_id=0, has_side_effects=True),
    )(
        observations, weights[0], gains, heads,
        pairing.reshape(1, rd), valid.reshape(1, rd),
    )
    return both[0, 0], both[1, 0]


def per_device(observations, weights, gains, heads, pairing, valid):
    rd = observations.shape[0]
    n = lax.axis_size("league")
    cap = 2 * rd // n
    fits = (
        n == 8 and cap % 16 == 0 and rd == 128
        and lax.axis_size("rep") == 4 and weights.shape[2] % TILE == 0
    )
    plan = kernel_plan if fits else gathered_plan
    return plan(observations, weights, gains, heads, pairing, valid)


def solution(mesh):
    return jax.shard_map(
        per_device,
        mesh=mesh,
        in_specs=(
            P(("league", "rep"), None),
            P("league", None, "rep"),
            P("league", None),
            P("league", "rep"),
            P(("league", "rep"), None),
            P(("league", "rep")),
        ),
        out_specs=(P(("league", "rep")), P(("league", "rep"))),
        check_vma=False,
    )
```

profile of v0, /device:TPU:0, one launch (start us, length us, event | category | flops | bytes accessed | tf_op | source)
XLA Modules:
  0.0 44.7 jit_solution(4920536054068523269)
XLA Ops:
  0.6 42.9 %shard_map.77 = f32[2,1,128]{2,1,0:T(1,128)} custom-call(bf16[128,2048]{1,0:T(8,128)(2,1)} %obs_hbm.1, bf16[2048,512]{1,0:T(8,128)(2,1)} %bitcast.7, f32[1,2048]{1,0:T(1,128)} %gain_ref.1, bf16[1,512]{1,0:T(2,128)(2,1)} %head_ref.1, s32[1,128]{1,0:T(1,128)} %bitcast.8, s32[1,128]{1,0:T(1,128)} %bitcast.9), custom_call_target="tpu_custom_call" | custom-call | tf_op jit(solution)/shard_map/pallas_call | solution.py:275
  43.5 1.2 %slice_bitcast_fusion = (f32[128]{0:T(128)}, f32[128]{0:T(128)}) fusion(f32[2,1,128]{2,1,0:T(1,128)} %shard_map.77), kind=kLoop, calls=%fused_computation | loop fusion | bytes 2048 | tf_op jit(solution)/shard_map/squeeze | solution.py:305
where the time goes:
time: 44.9 us; the launch traced here: 44.7 us
  Pallas kernels  42.9 us (96%)
  local copies, waits for them, and re-layouts  1.18 us (3%)
  between operations  0.64 us (1%)
    pallas_call x1, Pallas kernels, kernel_plan(): pl.pallas_call(functools.partial(kernel, n, cap), out_shape=jax.ShapeDtyp...  42.9 us
    squeeze x1, local copies, waits for them, and re-layouts, kernel_plan(): return (both[0, 0], both[1, 0])  1.18 us

commit v1 on v0

v1 whole, which is shorter than its diff:
```python
import functools

import jax
import jax.numpy as jnp
from jax import lax
from jax.experimental import pallas as pl
from jax.experimental.pallas import tpu as pltpu
from jax.sharding import PartitionSpec as P

MESH = pl.DeviceIdType.MESH
TILE = 512
PARTS = 4


def normed_values(obs_rows, agent_gain, weight_cols, head_cols):
    wide_rows = obs_rows.astype(jnp.float32)
    squares = jnp.mean(wide_rows * wide_rows, axis=1, keepdims=True)
    scaled = (wide_rows * lax.rsqrt(squares + 1e-06) * agent_gain).astype(jnp.bfloat16)
    hidden = jax.nn.silu(jnp.dot(scaled, weight_cols, preferred_element_type=jnp.float32))
    return jnp.sum(hidden * head_cols.astype(jnp.float32), axis=1)


def gathered_plan(observations, weights, gains, heads, pairing, valid):
    rows_dev, feature_width = observations.shape
    n_league = lax.axis_size("league")
    capacity = max(2, 2 * rows_dev // n_league)
    own_gain = gains[0]
    weight_full = lax.all_gather(weights[0], "rep", axis=1, tiled=True)
    head_full = lax.all_gather(heads[0], "rep", axis=0, tiled=True)
    own_value = normed_values(observations, own_gain, weight_full, head_full)
    owner_id = pairing[:, 0]
    is_live = valid == 1
    agent_iota = jnp.arange(n_league, dtype=jnp.int32)
    pick_table = ((owner_id[:, None] == agent_iota[None, :]) & is_live[:, None]).astype(jnp.float32)
    row_iota = jnp.arange(rows_dev, dtype=jnp.int32)
    earlier = (row_iota[:, None] > row_iota[None, :]).astype(jnp.float32)
    before = jnp.dot(earlier, pick_table, precision=lax.Precision.HIGHEST)
    slot_index = jnp.sum(before * pick_table, axis=1).astype(jnp.int32)
    target = jnp.where(is_live, owner_id * capacity + slot_index, n_league * capacity)
    outgoing = (
        jnp.zeros((n_league * capacity + 1, feature_width), jnp.bfloat16)
        .at[target]
        .set(observations)
    )
    outgoing = outgoing[: n_league * capacity].reshape(n_league, capacity, feature_width)
    received = lax.all_to_all(outgoing, "league", split_axis=0, concat_axis=0, tiled=True)
    flat_rows = received.reshape(received.shape[0] * received.shape[1], feature_width)
    answers = normed_values(flat_rows, own_gain, weight_full, head_full).reshape(
        received.shape[0], received.shape[1]
    )
    returned = lax.all_to_all(answers, "league", split_axis=0, concat_axis=0, tiled=True)
    flat_back = jnp.concatenate([returned.reshape(-1), jnp.zeros((1,), jnp.float32)])
    opponent_value = jnp.where(is_live, flat_back[target], 0.0)
    return (own_value, opponent_value)


def kernel(
    n, cap,
    obs_hbm, w_hbm, gain_hbm, head_hbm, pair_hbm, valid_hbm,
    out_ref,
    rows, wbuf, gain, head, pair, live, hv, code, slots, taken, distant, scaled, res, back, vown,
    lsem, asem, gsem, row_send, row_recv, slot_send, slot_recv, far_send, far_recv, back_send, back_recv,
):
    hs = n // 2
    rd, width = rows.shape[1], rows.shape[2]
    hid = wbuf.shape[2]
    span = width // PARTS
    lg = lax.axis_index("league")
    rp = lax.axis_index("rep")
    n_rep = lax.axis_size("rep")
    partner = lax.rem(rp + n_rep // 2, n_rep)
    sibling = rp + 1 - 2 * lax.rem(rp, 2)
    half = lg // hs
    pos = lax.rem(lg, hs)
    far_half = 1 - half
    zbit, y = pos // 2, lax.rem(pos, 2)
    inner = jnp.where(half + zbit == 1, 1, 0)
    level = half * hs + (1 - zbit) * 2 + y
    across = lg + 2 - 4 * half
    beside = lg + 1 - 2 * y

    def greet(sem, to):
        pl.semaphore_signal(sem, inc=1, device_id=to, device_id_type=MESH)

    barrier = pltpu.get_barrier_semaphore()

    @pl.when(inner == 1)
    def _():
        greet(barrier, (across, rp))

    for to in ((level, rp), (beside, rp), (lg, partner), (lg, sibling)):
        greet(barrier, to)

    def local(src, dst, which):
        return pltpu.make_async_copy(src, dst, lsem.at[which])

    copy_obs = local(obs_hbm, rows.at[0], 0)
    copy_w = local(w_hbm, wbuf.at[0], 1)
    copy_gain = local(gain_hbm, gain, 2)
    copy_head = local(head_hbm, head, 3)
    copy_pair = local(pair_hbm, pair, 4)
    copy_live = local(valid_hbm, live, 5)
    for move in (copy_pair, copy_live, copy_obs, copy_head, copy_w, copy_gain):
        move.start()

    sub = lax.broadcasted_iota(jnp.int32, (rd, rd), 0)
    lane = lax.broadcasted_iota(jnp.int32, (rd, rd), 1)
    agent_sub = lax.broadcasted_iota(jnp.int32, (n, rd), 0)

    def placing(agent):
        pick = jnp.where(agent == agent_sub, 1.0, 0.0)
        earlier = jnp.where(sub < lane, 1.0, 0.0).astype(jnp.bfloat16)
        before = jnp.dot(pick.astype(jnp.bfloat16), earlier, preferred_element_type=jnp.float32)
        slot = jnp.sum(before * pick, axis=0, keepdims=True).astype(jnp.int32)
        return pick, slot

    def choice(agent, slot, side):
        place = agent * cap + slot - side * rd
        return jnp.where(sub == place, 1.0, 0.0).astype(jnp.bfloat16)

    none = jnp.zeros((cap, width), jnp.bfloat16)
    taken[0, pos] = none
    taken[1, pos] = none
    back[0, lg] = jnp.zeros((1, rd), jnp.float32)
    back[1, lg] = jnp.zeros((1, rd), jnp.float32)
    copy_pair.wait()
    copy_live.wait()
    my_code = jnp.where(live[...] == 1, pair[...], -1)
    code[0] = my_code
    my_pick, my_slot = placing(my_code)
    my_far = choice(my_code, my_slot, far_half)
    my_near = choice(my_code, my_slot, half)
    copy_obs.wait()

    def fill(which, source, chosen, start, length):
        cols = pl.ds(start, length)
        picked = jnp.dot(chosen, rows[source, :, cols], preferred_element_type=jnp.float32)
        slots[which, :, :, cols] = picked.astype(jnp.bfloat16).reshape(hs, cap, length)

    fill(0, 0, my_far, 0, width)
    fill(1, 0, my_near, 0, width)
    copy_head.wait()
    hv[0] = head[...].astype(jnp.float32)

    def remote(src, dst, send, recv, to):
        return pltpu.make_async_remote_copy(
            src_ref=src, dst_ref=dst, send_sem=send, recv_sem=recv,
            device_id=to, device_id_type=MESH,
        )

    def cut(ref, part):
        return ref.at[:, pl.ds(part * span, span)]

    send_code = remote(code.at[0], code.at[1], asem.at[0, 0], asem.at[1, 0], (lg, partner))
    send_head = remote(hv.at[0], hv.at[1], asem.at[0, 1], asem.at[1, 1], (lg, sibling))
    send_w = remote(wbuf.at[0], wbuf.at[1], asem.at[0, 2], asem.at[1, 2], (lg, sibling))
    send_rows = [
        remote(cut(rows.at[0], p), cut(rows.at[1], p), row_send.at[p], row_recv.at[p], (lg, partner))
        for p in range(PARTS)
    ]

    def spot(u, side_y):
        return jnp.where(half == u, 2, 0) + side_y

    ys = (y, 1 - y)

    def far_copy(u, j, part):
        to = spot(u, ys[j])
        return remote(
            cut(slots.at[0, to], part), cut(distant.at[inner, y], part),
            far_send.at[0, u, j, part], far_recv.at[0, inner, y, part], (far_half * hs + to, rp),
        )

    def arrival(u, j, part):
        return remote(
            cut(slots.at[0, 0], part), cut(distant.at[u, ys[j]], part),
            far_send.at[0, 0, 0, part], far_recv.at[0, u, ys[j], part], (far_half * hs + spot(u, ys[j]), rp),
        )

    def forward_copy(u, j, part):
        return remote(
            cut(distant.at[u, ys[j]], part), cut(distant.at[u, 2 + ys[j]], part),
            far_send.at[1, u, j, part], far_recv.at[1, u, ys[j], part], (lg, partner),
        )

    def landing(u, j, part):
        return remote(
            cut(distant.at[u, ys[j]], part), cut(distant.at[u, 2 + ys[j]], part),
            far_send.at[1, u, j, part], far_recv.at[1, u, ys[j], part], (lg, partner),
        )

    near_to = ((zbit * 2 + 1 - y), ((1 - zbit) * 2 + y), ((1 - zbit) * 2 + 1 - y))

    def near_copy(kind, k, part):
        to = near_to[k]
        return remote(
            cut(slots.at[1 + kind, to], part), cut(taken.at[kind, pos], part),
            slot_send.at[kind, k, part], slot_recv.at[kind, k, part], (half * hs + to, rp),
        )

    def near_whole(k):
        to = near_to[k]
        return remote(
            slots.at[1, to], taken.at[0, pos],
            slot_send.at[0, k, 0], slot_recv.at[0, k, 0], (half * hs + to, rp),
        )

    near0 = [near_whole(k) for k in range(3)]
    near2 = [near_copy(1, k, p) for p in range(PARTS) for k in range(3)]
    far = {(u, j, p): far_copy(u, j, p) for u in range(2) for j in range(2) for p in range(PARTS)}
    onward = {(u, j, p): forward_copy(u, j, p) for u in range(2) for j in range(2) for p in range(PARTS)}

    def send_far(u, j):
        for p in range(PARTS):
            far[u, j, p].start()

    pl.semaphore_wait(barrier, 4 + inner)
    greet(gsem.at[0], (level, rp))

    @pl.when(inner == 1)
    def _():
        greet(gsem.at[1], (across, rp))
        send_far(1, 0)

    send_code.start()
    for move in send_rows:
        move.start()
    near0[0].start()
    near0[1].start()
    copy_w.wait()
    send_head.start()
    send_w.start()
    pl.semaphore_wait(gsem.at[0], 1)

    @pl.when(inner == 1)
    def _():
        pl.semaphore_wait(gsem.at[1], 1)
        greet(gsem.at[2], (level, rp))
        greet(gsem.at[2], (across, rp))
        send_far(0, 0)
        send_far(1, 1)

    @pl.when(inner == 0)
    def _():
        send_far(1, 0)

    near0[2].start()
    pl.semaphore_wait(gsem.at[2], 1)

    @pl.when(inner == 1)
    def _():
        greet(gsem.at[3], (level, rp))
        send_far(0, 1)

    @pl.when(inner == 0)
    def _():
        send_far(0, 0)
        send_far(1, 1)
        pl.semaphore_wait(gsem.at[3], 1)
        send_far(0, 1)

    copy_gain.wait()

    def values(block):
        wide = block.astype(jnp.float32)
        squares = jnp.mean(wide * wide, axis=1, keepdims=True)
        scaled[...] = (wide * lax.rsqrt(squares + 1e-06) * gain[...]).astype(jnp.bfloat16)
        acc = jnp.zeros((rd, rd), jnp.float32)
        for j in range(2):
            for col in range(0, hid, TILE):
                v = jnp.dot(scaled[...], wbuf[j, :, pl.ds(col, TILE)], preferred_element_type=jnp.float32)
                part = v / (1.0 + jnp.exp(-v)) * hv[j, :, pl.ds(col, TILE)]
                for c in range(0, TILE, rd):
                    acc = acc + part[:, c:c + rd]
        return jnp.sum(acc.T, axis=0, keepdims=True)

    replies = []

    def reply(line, index, side, link, to):
        move = remote(
            res.at[line], back.at[side, lg], back_send.at[side, index], back_recv.at[side, link], to,
        )
        move.start()
        replies.append(move)

    def forward(u, j):
        for p in range(PARTS):
            arrival(u, j, p).wait_recv()
            onward[u, j, p].start()

    def answer_near(kind):
        res[kind] = values(taken[kind].reshape(rd, width))
        who = rp if kind == 0 else partner
        for k in range(3):
            reply(kind, k, kind, k, (half * hs + near_to[k], who))

    def answer_far(u):
        for j in range(2):
            for p in range(PARTS):
                landing(u, j, p).wait_recv()
        found = values(distant[u].reshape(rd, width))
        res[2 + 2 * u] = found
        res[3 + 2 * u] = pltpu.roll(found, rd // 2, 1)
        for j in range(2):
            to = far_half * hs + spot(u, ys[j])
            link = 3 + 2 * inner + j
            reply(3 + 2 * u, 3 + 2 * u + j, 1, link, (to, partner))
            reply(2 + 2 * u, 3 + 2 * u + j, 0, link, (to, rp))

    send_head.wait_recv()
    send_w.wait_recv()
    mine = values(rows[0])

    send_code.wait_recv()
    other_code = code[1]
    other_near = choice(other_code, placing(other_code)[1], half)
    for p in range(PARTS):
        send_rows[p].wait_recv()
        fill(2, 1, other_near, p * span, span)
        for k in range(3):
            near2[p * 3 + k].start()
        if p == PARTS - 2:
            forward(0, 0)
    vown[0] = values(rows[1])
    send_own = remote(vown.at[0], vown.at[1], asem.at[0, 3], asem.at[1, 3], (lg, partner))
    send_own.start()
    forward(0, 1)
    for move in near0:
        move.wait_recv()
    answer_near(0)
    forward(1, 0)
    for move in near2:
        move.wait_recv()
    answer_near(1)
    answer_far(0)
    forward(1, 1)
    answer_far(1)

    send_own.wait_recv()
    own = mine + vown[1]
    out_ref[0] = own
    for side in range(2):
        for link in range(7):
            remote(
                res.at[0], back.at[side, lg], back_send.at[side, 0], back_recv.at[side, link], (lg, partner),
            ).wait_recv()
    table = jnp.concatenate([back[0, a] + back[1, a] for a in range(n)], axis=0)
    base = jnp.where(my_code // hs == half, pos, y) * cap
    chosen = jnp.where(sub == my_slot + base, 1.0, 0.0)
    found = jnp.dot(table, chosen, preferred_element_type=jnp.float32, precision=lax.Precision.HIGHEST)
    opp = jnp.sum(jnp.where(my_pick > 0.0, found, 0.0), axis=0, keepdims=True)
    out_ref[1] = jnp.where(my_code == lg, own, opp)
    for move in [send_code, send_head, send_w, send_own, *send_rows, *near0, *near2, *far.values(), *onward.values(), *replies]:
        move.wait_send()


def kernel_plan(observations, weights, gains, heads, pairing, valid):
    rd, width = observations.shape
    hid = weights.shape[2]
    n = lax.axis_size("league")
    cap = 2 * rd // n
    hs = n // 2
    vmem = pl.BlockSpec(memory_space=pltpu.VMEM)
    anywhere = pl.BlockSpec(memory_space=pl.ANY)
    both = pl.pallas_call(
        functools.partial(kernel, n, cap),
        out_shape=jax.ShapeDtypeStruct((2, 1, rd), jnp.float32),
        in_specs=[anywhere] * 6,
        out_specs=vmem,
        scratch_shapes=[
            pltpu.VMEM((2, rd, width), jnp.bfloat16),
            pltpu.VMEM((2, width, hid), jnp.bfloat16),
            pltpu.VMEM((1, width), jnp.float32),
            pltpu.VMEM((1, hid), jnp.bfloat16),
            pltpu.VMEM((1, rd), jnp.int32),
            pltpu.VMEM((1, rd), jnp.int32),
            pltpu.VMEM((2, 1, hid), jnp.float32),
            pltpu.VMEM((2, 1, rd), jnp.int32),
            pltpu.VMEM((3, hs, cap, width), jnp.bfloat16),
            pltpu.VMEM((2, hs, cap, width), jnp.bfloat16),
            pltpu.VMEM((2, hs, cap, width), jnp.bfloat16),
            pltpu.VMEM((rd, width), jnp.bfloat16),
            pltpu.VMEM((6, 1, rd), jnp.float32),
            pltpu.VMEM((2, n, 1, rd), jnp.float32),
            pltpu.VMEM((2, 1, rd), jnp.float32),
            pltpu.SemaphoreType.DMA((6,)),
            pltpu.SemaphoreType.DMA((2, 4)),
            pltpu.SemaphoreType.REGULAR((4,)),
            pltpu.SemaphoreType.DMA((PARTS,)),
            pltpu.SemaphoreType.DMA((PARTS,)),
            pltpu.SemaphoreType.DMA((2, 3, PARTS)),
            pltpu.SemaphoreType.DMA((2, 3, PARTS)),
            pltpu.SemaphoreType.DMA((2, 2, 2, PARTS)),
            pltpu.SemaphoreType.DMA((2, 2, 2, PARTS)),
            pltpu.SemaphoreType.DMA((2, 7)),
            pltpu.SemaphoreType.DMA((2, 7)),
        ],
        compiler_params=pltpu.CompilerParams(collective_id=0, has_side_effects=True),
    )(
        observations, weights[0], gains, heads,
        pairing.reshape(1, rd), valid.reshape(1, rd),
    )
    return both[0, 0], both[1, 0]


def per_device(observations, weights, gains, heads, pairing, valid):
    rd = observations.shape[0]
    n = lax.axis_size("league")
    cap = 2 * rd // n
    fits = (
        n == 8 and cap % 16 == 0 and rd == 128
        and lax.axis_size("rep") == 4 and weights.shape[2] % TILE == 0
    )
    plan = kernel_plan if fits else gathered_plan
    return plan(observations, weights, gains, heads, pairing, valid)


def solution(mesh):
    return jax.shard_map(
        per_device,
        mesh=mesh,
        in_specs=(
            P(("league", "rep"), None),
            P("league", None, "rep"),
            P("league", None),
            P("league", "rep"),
            P(("league", "rep"), None),
            P(("league", "rep")),
        ),
        out_specs=(P(("league", "rep")), P(("league", "rep"))),
        check_vma=False,
    )
```

time: 44.9 us -> 42.6 us (0.949)
  the two profiles are of different devices: /device:TPU:0 before, /device:TPU:8 now
where the time goes in v1:
time: 42.6 us; the launch traced here: 42.4 us
  Pallas kernels  40.6 us (95%)
  local copies, waits for them, and re-layouts  1.18 us (3%)
  between operations  0.64 us (2%)
    pallas_call x1, Pallas kernels, kernel_plan(): pl.pallas_call(functools.partial(kernel, n, cap), out_shape=jax.ShapeDtyp...  40.6 us
    squeeze x1, local copies, waits for them, and re-layouts, kernel_plan(): return (both[0, 0], both[1, 0])  1.18 us

profile of v1, /device:TPU:8, one launch (start us, length us, event | category | flops | bytes accessed | tf_op | source)
XLA Modules:
  0.0 42.4 jit_solution(15660188365347758585)
XLA Ops:
  0.6 40.6 %shard_map.77 = f32[2,1,128]{2,1,0:T(1,128)} custom-call(bf16[128,2048]{1,0:T(8,128)(2,1)} %obs_hbm.1, bf16[2048,512]{1,0:T(8,128)(2,1)} %bitcast.7, f32[1,2048]{1,0:T(1,128)} %gain_hbm.1, bf16[1,512]{1,0:T(2,128)(2,1)} %head_hbm.1, s32[1,128]{1,0:T(1,128)} %bitcast.8, s32[1,128]{1,0:T(1,128)} %bitcast.9), custom_call_target="tpu_custom_call" | custom-call | tf_op jit(solution)/shard_map/pallas_call | solution.py:365
  41.2 1.2 %slice_bitcast_fusion = (f32[128]{0:T(128)}, f32[128]{0:T(128)}) fusion(f32[2,1,128]{2,1,0:T(1,128)} %shard_map.77), kind=kLoop, calls=%fused_computation | loop fusion | bytes 2048 | tf_op jit(solution)/shard_map/squeeze | solution.py:403

commit v2 on v1

--- a/solution.py
+++ b/solution.py
@@ -59,7 +59,7 @@
     obs_hbm, w_hbm, gain_hbm, head_hbm, pair_hbm, valid_hbm,
     out_ref,
     rows, wbuf, gain, head, pair, live, hv, code, slots, taken, distant, scaled, res, back, vown,
-    lsem, asem, gsem, row_send, row_recv, slot_send, slot_recv, far_send, far_recv, back_send, back_recv,
+    lsem, gsem, sent, came, row_came, far_came,
 ):
     hs = n // 2
     rd, width = rows.shape[1], rows.shape[2]
@@ -151,11 +151,11 @@
     def cut(ref, part):
         return ref.at[:, pl.ds(part * span, span)]
 
-    send_code = remote(code.at[0], code.at[1], asem.at[0, 0], asem.at[1, 0], (lg, partner))
-    send_head = remote(hv.at[0], hv.at[1], asem.at[0, 1], asem.at[1, 1], (lg, sibling))
-    send_w = remote(wbuf.at[0], wbuf.at[1], asem.at[0, 2], asem.at[1, 2], (lg, sibling))
+    send_code = remote(code.at[0], code.at[1], sent.at[0], came.at[0], (lg, partner))
+    send_head = remote(hv.at[0], hv.at[1], sent.at[1], came.at[1], (lg, sibling))
+    send_w = remote(wbuf.at[0], wbuf.at[1], sent.at[2], came.at[2], (lg, sibling))
     send_rows = [
-        remote(cut(rows.at[0], p), cut(rows.at[1], p), row_send.at[p], row_recv.at[p], (lg, partner))
+        remote(cut(rows.at[0], p), cut(rows.at[1], p), sent.at[3], row_came.at[p], (lg, partner))
         for p in range(PARTS)
     ]
 
@@ -168,25 +168,19 @@
         to = spot(u, ys[j])
         return remote(
             cut(slots.at[0, to], part), cut(distant.at[inner, y], part),
-            far_send.at[0, u, j, part], far_recv.at[0, inner, y, part], (far_half * hs + to, rp),
+            sent.at[4], far_came.at[inner, y, part], (far_half * hs + to, rp),
         )
 
     def arrival(u, j, part):
         return remote(
             cut(slots.at[0, 0], part), cut(distant.at[u, ys[j]], part),
-            far_send.at[0, 0, 0, part], far_recv.at[0, u, ys[j], part], (far_half * hs + spot(u, ys[j]), rp),
+            sent.at[4], far_came.at[u, ys[j], part], (far_half * hs + spot(u, ys[j]), rp),
         )
 
     def forward_copy(u, j, part):
         return remote(
             cut(distant.at[u, ys[j]], part), cut(distant.at[u, 2 + ys[j]], part),
-            far_send.at[1, u, j, part], far_recv.at[1, u, ys[j], part], (lg, partner),
-        )
-
-    def landing(u, j, part):
-        return remote(
-            cut(distant.at[u, ys[j]], part), cut(distant.at[u, 2 + ys[j]], part),
-            far_send.at[1, u, j, part], far_recv.at[1, u, ys[j], part], (lg, partner),
+            sent.at[5], came.at[4 + u], (lg, partner),
         )
 
     near_to = ((zbit * 2 + 1 - y), ((1 - zbit) * 2 + y), ((1 - zbit) * 2 + 1 - y))
@@ -195,15 +189,18 @@
         to = near_to[k]
         return remote(
             cut(slots.at[1 + kind, to], part), cut(taken.at[kind, pos], part),
-            slot_send.at[kind, k, part], slot_recv.at[kind, k, part], (half * hs + to, rp),
+            sent.at[7], came.at[7], (half * hs + to, rp),
         )
 
     def near_whole(k):
         to = near_to[k]
         return remote(
             slots.at[1, to], taken.at[0, pos],
-            slot_send.at[0, k, 0], slot_recv.at[0, k, 0], (half * hs + to, rp),
-        )
+            sent.at[6], came.at[6], (half * hs + to, rp),
+        )
+
+    def whole(ref, out, into):
+        return remote(ref, ref, sent.at[out], came.at[into], (lg, partner))
 
     near0 = [near_whole(k) for k in range(3)]
     near2 = [near_copy(1, k, p) for p in range(PARTS) for k in range(3)]
@@ -238,7 +235,6 @@
         greet(gsem.at[2], (level, rp))
         greet(gsem.at[2], (across, rp))
         send_far(0, 0)
-        send_far(1, 1)
 
     @pl.when(inner == 0)
     def _():
@@ -251,6 +247,7 @@
     def _():
         greet(gsem.at[3], (level, rp))
         send_far(0, 1)
+        send_far(1, 1)
 
     @pl.when(inner == 0)
     def _():
@@ -274,17 +271,11 @@
                     acc = acc + part[:, c:c + rd]
         return jnp.sum(acc.T, axis=0, keepdims=True)
 
-    replies = []
-
-    def reply(line, index, side, link, to):
-        move = remote(
-            res.at[line], back.at[side, lg], back_send.at[side, index], back_recv.at[side, link], to,
-        )
-        move.start()
-        replies.append(move)
-
-    def forward(u, j):
-        for p in range(PARTS):
+    def reply(line, side, to):
+        remote(res.at[line], back.at[side, lg], sent.at[0], came.at[8], to).start()
+
+    def forward(u, j, first, last):
+        for p in range(first, last):
             arrival(u, j, p).wait_recv()
             onward[u, j, p].start()
 
@@ -292,20 +283,17 @@
         res[kind] = values(taken[kind].reshape(rd, width))
         who = rp if kind == 0 else partner
         for k in range(3):
-            reply(kind, k, kind, k, (half * hs + near_to[k], who))
+            reply(kind, kind, (half * hs + near_to[k], who))
 
     def answer_far(u):
-        for j in range(2):
-            for p in range(PARTS):
-                landing(u, j, p).wait_recv()
+        whole(distant.at[u, pl.ds(0, 2)], 5, 4 + u).wait_recv()
         found = values(distant[u].reshape(rd, width))
         res[2 + 2 * u] = found
         res[3 + 2 * u] = pltpu.roll(found, rd // 2, 1)
         for j in range(2):
             to = far_half * hs + spot(u, ys[j])
-            link = 3 + 2 * inner + j
-            reply(3 + 2 * u, 3 + 2 * u + j, 1, link, (to, partner))
-            reply(2 + 2 * u, 3 + 2 * u + j, 0, link, (to, rp))
+            reply(3 + 2 * u, 1, (to, partner))
+            reply(2 + 2 * u, 0, (to, rp))
 
     send_head.wait_recv()
     send_w.wait_recv()
@@ -320,38 +308,36 @@
         for k in range(3):
             near2[p * 3 + k].start()
         if p == PARTS - 2:
-            forward(0, 0)
+            forward(1, 0, 0, 2)
+            forward(0, 0, 0, PARTS)
     vown[0] = values(rows[1])
-    send_own = remote(vown.at[0], vown.at[1], asem.at[0, 3], asem.at[1, 3], (lg, partner))
+    send_own = remote(vown.at[0], vown.at[1], sent.at[0], came.at[3], (lg, partner))
     send_own.start()
-    forward(0, 1)
-    for move in near0:
-        move.wait_recv()
+    forward(1, 0, 2, PARTS)
+    forward(0, 1, 0, PARTS)
+    whole(taken.at[0, pl.ds(0, 3)], 6, 6).wait_recv()
     answer_near(0)
-    forward(1, 0)
-    for move in near2:
-        move.wait_recv()
+    forward(1, 1, 0, PARTS)
+    answer_far(0)
+    whole(taken.at[1, pl.ds(0, 3)], 7, 7).wait_recv()
     answer_near(1)
-    answer_far(0)
-    forward(1, 1)
     answer_far(1)
 
     send_own.wait_recv()
     own = mine + vown[1]
     out_ref[0] = own
-    for side in range(2):
-        for link in range(7):
-            remote(
-                res.at[0], back.at[side, lg], back_send.at[side, 0], back_recv.at[side, link], (lg, partner),
-            ).wait_recv()
+    whole(back.at[:, pl.ds(0, n - 1)], 0, 8).wait_recv()
     table = jnp.concatenate([back[0, a] + back[1, a] for a in range(n)], axis=0)
     base = jnp.where(my_code // hs == half, pos, y) * cap
     chosen = jnp.where(sub == my_slot + base, 1.0, 0.0)
     found = jnp.dot(table, chosen, preferred_element_type=jnp.float32, precision=lax.Precision.HIGHEST)
     opp = jnp.sum(jnp.where(my_pick > 0.0, found, 0.0), axis=0, keepdims=True)
     out_ref[1] = jnp.where(my_code == lg, own, opp)
-    for move in [send_code, send_head, send_w, send_own, *send_rows, *near0, *near2, *far.values(), *onward.values(), *replies]:
-        move.wait_send()
+    for ref, out in (
+        (back, 0), (hv.at[0], 1), (wbuf.at[0], 2), (rows.at[0], 3), (slots.at[0], 4), (slots.at[0], 5),
+        (slots.at[1, pl.ds(0, 3)], 6), (slots.at[2, pl.ds(0, 3)], 7),
+    ):
+        whole(ref, out, 0).wait_send()
 
 
 def kernel_plan(observations, weights, gains, heads, pairing, valid):
@@ -384,16 +370,11 @@
             pltpu.VMEM((2, n, 1, rd), jnp.float32),
             pltpu.VMEM((2, 1, rd), jnp.float32),
             pltpu.SemaphoreType.DMA((6,)),
-            pltpu.SemaphoreType.DMA((2, 4)),
             pltpu.SemaphoreType.REGULAR((4,)),
+            pltpu.SemaphoreType.DMA((8,)),
+            pltpu.SemaphoreType.DMA((9,)),
             pltpu.SemaphoreType.DMA((PARTS,)),
-            pltpu.SemaphoreType.DMA((PARTS,)),
-            pltpu.SemaphoreType.DMA((2, 3, PARTS)),
-            pltpu.SemaphoreType.DMA((2, 3, PARTS)),
-            pltpu.SemaphoreType.DMA((2, 2, 2, PARTS)),
-            pltpu.SemaphoreType.DMA((2, 2, 2, PARTS)),
-            pltpu.SemaphoreType.DMA((2, 7)),
-            pltpu.SemaphoreType.DMA((2, 7)),
+            pltpu.SemaphoreType.DMA((2, 2, PARTS)),
         ],
         compiler_params=pltpu.CompilerParams(collective_id=0, has_side_effects=True),
     )(

time: 42.6 us -> 38.9 us (0.913)
  the two profiles are of different devices: /device:TPU:8 before, /device:TPU:0 now
where the time goes in v2:
time: 38.9 us; the launch traced here: 38.7 us
  Pallas kernels  36.9 us (95%)
  local copies, waits for them, and re-layouts  1.18 us (3%)
  between operations  0.64 us (2%)
    pallas_call x1, Pallas kernels, kernel_plan(): pl.pallas_call(functools.partial(kernel, n, cap), out_shape=jax.ShapeDtyp...  36.9 us
    squeeze x1, local copies, waits for them, and re-layouts, kernel_plan(): return (both[0, 0], both[1, 0])  1.18 us

profile of v2, /device:TPU:0, one launch (start us, length us, event | category | flops | bytes accessed | tf_op | source)
XLA Modules:
  0.0 38.7 jit_solution(12213634282795700997)
XLA Ops:
  0.6 36.9 %shard_map.77 = f32[2,1,128]{2,1,0:T(1,128)} custom-call(bf16[128,2048]{1,0:T(8,128)(2,1)} %obs_hbm.1, bf16[2048,512]{1,0:T(8,128)(2,1)} %bitcast.7, f32[1,2048]{1,0:T(1,128)} %gain_hbm.1, bf16[1,512]{1,0:T(2,128)(2,1)} %head_hbm.1, s32[1,128]{1,0:T(1,128)} %bitcast.8, s32[1,128]{1,0:T(1,128)} %bitcast.9), custom_call_target="tpu_custom_call" | custom-call | tf_op jit(solution)/shard_map/pallas_call | solution.py:351
  37.6 1.2 %slice_bitcast_fusion = (f32[128]{0:T(128)}, f32[128]{0:T(128)}) fusion(f32[2,1,128]{2,1,0:T(1,128)} %shard_map.77), kind=kLoop, calls=%fused_computation | loop fusion | bytes 2048 | tf_op jit(solution)/shard_map/squeeze | solution.py:384
